TPU v7x, 32 devices: a whole 2x2x4 slice. The times are simulated.
32 devices in a mesh: fsdp: 8 (over z, y), dom: 4 (over x, core).
Axes of the slice: x: 2, y: 2, z: 4, core: 2. Of those that a mesh axis runs over, the one named last changes fastest.
Arguments:
- hidden_states: bfloat16 [256, 128, 768], P(('fsdp', 'dom')), may hold values from -40 to 40
- title_tokens: int32 [256, 128], P(('fsdp', 'dom')), may hold values from 0 to 30521, as said below
- query_key_value: bfloat16 [768, 2304], P('fsdp'), may hold values from -0.5 to 2.5
- output_weight: bfloat16 [768, 768], P('fsdp'), may hold values from -0.21875 to 0.21875
- up_weight: bfloat16 [768, 3072], P('fsdp'), may hold values from -0.21875 to 0.21875
- down_weight: bfloat16 [3072, 768], P('fsdp'), may hold values from -0.109375 to 0.109375
- attention_gain: float32 [768], replicated, may hold values from 0.25 to 1.75
- feedforward_gain: float32 [768], replicated, may hold values from 0.25 to 1.75
- encoded: bfloat16 [16384, 768], P(('fsdp', 'dom')), may hold values from -6 to 6
- send_rows: int32 [32, 32, 48], P(('fsdp', 'dom')), may hold values from 0 to 511
- send_count: int32 [32, 32], P(('fsdp', 'dom')), may hold values from 6 to 48, as said below
- arrival_nodes: int32 [32, 32, 48], P(('fsdp', 'dom')), may hold values from 0 to 511
- sage_weight: bfloat16 [2, 768, 1024], P(None, 'fsdp'), may hold values from -0.21875 to 0.21875
- node_gain: float32 [1024], replicated, may hold values from 0.25 to 1.75
Outputs:
- title_vectors: bfloat16 [256, 768], P(('fsdp', 'dom'))
- node_output: bfloat16 [16384, 1024], P(('fsdp', 'dom'))
Inputs may be any that keep to these rules, and one draw needn't show every extreme that they name: `title_tokens`: in each title the nonzero ids come first and zeros fill the rest; at least 16 ids of every title are nonzero. `send_count`: in every draw some device receives exactly 48 valid slots from every device.
All inputs are finite; a program needn't handle non-finite values.
Results may differ from a plain program's by a relative error of at most 0.0056.
Values may be sent and summed in bfloat16 or wider, within the bound.
A program may use at most 192 MiB of HBM per device.

v0:
```python
import math
import jax
import jax.numpy as jnp
from jax import lax
from jax.sharding import PartitionSpec as P

HEADS = 12
HEAD_DIM = 64
LN_EPSILON = 1e-12


def layer_norm(values, gain):
    center = values - jnp.mean(values, axis=-1, keepdims=True)
    spread = jnp.mean(center * center, axis=-1, keepdims=True)
    return center * lax.rsqrt(spread + LN_EPSILON) * gain


def encode_titles(
    hidden_states,
    title_tokens,
    query_key_value,
    output_weight,
    up_weight,
    down_weight,
    attention_gain,
    feedforward_gain,
):
    titles, seq_len, width = hidden_states.shape
    flat = hidden_states.reshape(titles * seq_len, width)
    live = title_tokens != 0
    full_project, full_output = (
        lax.all_gather(query_key_value, "fsdp", axis=0, tiled=True),
        lax.all_gather(output_weight, "fsdp", axis=0, tiled=True),
    )
    projected = jnp.dot(flat, full_project, preferred_element_type=jnp.float32).astype(jnp.bfloat16)
    projected = projected.reshape(titles, seq_len, 3, HEADS, HEAD_DIM)
    query_states = projected[:, :, 0]
    key_states = projected[:, :, 1]
    value_states = projected[:, :, 2]
    scores = jnp.einsum(
        "tihd,tjhd->thij", query_states, key_states, preferred_element_type=jnp.float32
    )
    scores = scores * (1.0 / math.sqrt(HEAD_DIM))
    scores = jnp.where(live[:, None, None, :], scores, -jnp.inf)
    highest = jnp.max(scores, axis=-1, keepdims=True)
    weights = jnp.exp(scores - highest)
    probs = (weights / jnp.sum(weights, axis=-1, keepdims=True)).astype(jnp.bfloat16)
    context = jnp.einsum("thij,tjhd->tihd", probs, value_states, preferred_element_type=jnp.float32)
    context = context.astype(jnp.bfloat16).reshape(titles * seq_len, width)
    mixed = jnp.dot(context, full_output, preferred_element_type=jnp.float32)
    attended = layer_norm(flat.astype(jnp.float32) + mixed, attention_gain).astype(jnp.bfloat16)
    attended = lax.optimization_barrier(attended)
    full_up, full_down = (
        lax.all_gather(up_weight, "fsdp", axis=0, tiled=True),
        lax.all_gather(down_weight, "fsdp", axis=0, tiled=True),
    )
    inner = jax.nn.gelu(
        jnp.dot(attended, full_up, preferred_element_type=jnp.float32), approximate=False
    )
    inner = inner.astype(jnp.bfloat16)
    lowered = jnp.dot(inner, full_down, preferred_element_type=jnp.float32)
    token_out = layer_norm(attended.astype(jnp.float32) + lowered, feedforward_gain).reshape(
        titles, seq_len, width
    )
    live_weight = live.astype(jnp.float32)
    pooled = jnp.sum(token_out * live_weight[:, :, None], axis=1) / jnp.sum(
        live_weight, axis=1, keepdims=True
    )
    return pooled.astype(jnp.bfloat16)


def scatter_sums(arrived, targets, valid, nodes):
    width = arrived.shape[2]
    mask_flat = valid.reshape(-1).astype(jnp.float32)
    label_flat = targets.reshape(-1)
    rows = arrived.reshape(-1, width).astype(jnp.float32) * mask_flat[:, None]
    sums = jax.ops.segment_sum(rows, label_flat, num_segments=nodes)
    degree = jax.ops.segment_sum(mask_flat, label_flat, num_segments=nodes)
    return (sums, degree)


def on_device(
    hidden_states,
    title_tokens,
    query_key_value,
    output_weight,
    up_weight,
    down_weight,
    attention_gain,
    feedforward_gain,
    encoded,
    send_rows,
    send_count,
    arrival_nodes,
    sage_weight,
    node_gain,
):
    titles = hidden_states.shape[0]
    nodes, width = encoded.shape
    outgoing = jnp.take(encoded, send_rows[0], axis=0)
    slot_count = outgoing.shape[1]
    counts_out = send_count[0].astype(jnp.bfloat16)
    arrived, arrived_counts = (
        lax.all_to_all(outgoing, ("fsdp", "dom"), split_axis=0, concat_axis=0, tiled=True),
        lax.all_to_all(counts_out, ("fsdp", "dom"), split_axis=0, concat_axis=0, tiled=True),
    )
    valid = (
        jnp.arange(slot_count, dtype=jnp.int32)[None, :] < arrived_counts.astype(jnp.int32)[:, None]
    )
    targets = arrival_nodes[0]
    title_vectors = encode_titles(
        hidden_states,
        title_tokens,
        query_key_value,
        output_weight,
        up_weight,
        down_weight,
        attention_gain,
        feedforward_gain,
    )
    sums, degree = scatter_sums(arrived, targets, valid, nodes)
    neighbour_mean = (sums / jnp.maximum(degree, 1.0)[:, None]).astype(jnp.bfloat16)
    self_rows = jnp.concatenate([title_vectors, encoded[titles:]], axis=0)
    piece = lax.all_gather(sage_weight, "fsdp", axis=1, tiled=True)
    running = jnp.dot(self_rows, piece[0], preferred_element_type=jnp.float32)
    combined = running + jnp.dot(neighbour_mean, piece[1], preferred_element_type=jnp.float32)
    node_output = layer_norm(combined, node_gain).astype(jnp.bfloat16)
    return (title_vectors, node_output)


def solution(mesh):
    return jax.shard_map(
        on_device,
        mesh=mesh,
        in_specs=(
            P(("fsdp", "dom"), None, None),
            P(("fsdp", "dom"), None),
            P("fsdp", None),
            P("fsdp", None),
            P("fsdp", None),
            P("fsdp", None),
            P(),
            P(),
            P(("fsdp", "dom"), None),
            P(("fsdp", "dom"), None, None),
            P(("fsdp", "dom"), None),
            P(("fsdp", "dom"), None, None),
            P(None, "fsdp", None),
            P(),
        ),
        out_specs=(P(("fsdp", "dom"), None), P(("fsdp", "dom"), None)),
        check_vma=False,
    )
```

profile of v0, /device:TPU:0, one launch (start us, length us, event | category | flops | bytes accessed | tf_op | source)
XLA Modules:
  0.0 387.3 jit_solution(11818364927257436339)
XLA Ops:
  7.2 0.7 all-gather.6.cloned.1.call-update
  8.0 0.7 all-gather.8.cloned.1.call-update
  8.7 0.7 all-gather.10.cloned.1.call-update
  10.6 0.7 copy.50
  11.3 7.3 %all-to-all-start.1 = ((bf16[32,1,1]{2,1,0:T(2,128)(2,1)}), bf16[32,1,1]{2,1,0:T(2,128)(2,1)S(1)}, u32[]{:S(2)}, u32[]{:S(2)}) async-start(bf16[32,1,1]{2,1,0:T(2,128)(2,1)} %copy.50), calls=%async_computation.1 | async-start | bytes 32768 | tf_op jit(solution)/shard_map/all_to_all | solution.py:105
  18.7 0.7 compare_select_fusion
  19.5 5.0 %gather_fusion = bf16[1536,768]{1,0:T(8,128)(2,1)S(1)} fusion(bf16[512,768]{1,0:T(8,128)(2,1)S(1)} %copy-done, s32[2048]{0:T(1024)S(1)} %pad_clamp_fusion), kind=kCustom, calls=%fused_computation | custom fusion | bytes 4724736 | tf_op jit(solution)/shard_map/jit(_take)/gather | solution.py:100
  24.5 1.7 broadcast_select_fusion
  26.2 5.8 %all-to-all-start = ((bf16[32,48,768]{2,1,0:T(8,128)(2,1)}), bf16[32,48,768]{2,1,0:T(8,128)(2,1)S(1)}, u32[]{:S(2)}, u32[]{:S(2)}) async-start(bf16[32,48,768]{2,1,0:T(8,128)(2,1)} %broadcast_select_fusion), calls=%async_computation | async-start | bytes 4718592 | tf_op jit(solution)/shard_map/all_to_all | solution.py:104
  32.7 2.6 copy.54
  35.5 0.7 convert_reduce_fusion
  36.3 11.1 %scatter_custom_fusion.1 = f32[512]{0:T(512)S(1)} fusion(s32[1536]{0:T(1024)S(1)} %reshape.151, f32[1536]{0:T(1024)S(1)} %reshape.161, f32[]{:T(128)} %constant.42.clone.1), kind=kCustom, calls=%fused_computation.81 | custom fusion | flops 1536 | bytes 2052 | tf_op jit(solution)/shard_map/scatter-add | solution.py:78
  47.5 70.7 %all-to-all-done = bf16[32,48,768]{2,1,0:T(8,128)(2,1)S(1)} async-done(((bf16[32,48,768]{2,1,0:T(8,128)(2,1)}), bf16[32,48,768]{2,1,0:T(8,128)(2,1)S(1)}, u32[]{:S(2)}, u32[]{:S(2)}) %all-to-all-start) | async-done | bytes 2359328 | tf_op jit(solution)/shard_map/all_to_all | solution.py:104
  118.2 12.9 %scatter_custom_fusion = f32[512,768]{1,0:T(8,128)} fusion(s32[1536]{0:T(1024)S(1)} %reshape.151, bf16[1536,768]{1,0:T(8,128)(2,1)S(1)} %bitcast.72, f32[1536]{0:T(1024)S(1)} %reshape.161, f32[]{:T(128)} %constant.42.clone.1), kind=kCustom, calls=%fused_computation.30 | custom fusion | flops 3538944 | bytes 3940356 | tf_op jit(solution)/shard_map/scatter-add | solution.py:77
  131.1 8.5 %convolution_convert_fusion = bf16[1024,2304]{1,0:T(8,128)(2,1)} fusion(bf16[1024,768]{1,0:T(8,128)(2,1)} %bitcast.74, bf16[768,2304]{1,0:T(8,128)(2,1)} %all-gather.6.cloned.1.call-done), kind=kOutput, calls=%fused_computation.27 | convolution fusion | flops 3626237952 | bytes 9830400 | tf_op jit(solution)/shard_map/dot_general | solution.py:35
  139.7 6.7 %copy.42 = bf16[1024,2304]{0,1:T(8,128)(2,1)} copy(bf16[1024,2304]{1,0:T(8,128)(2,1)} %convolution_convert_fusion) | data formatting | bytes 9437184 | tf_op jit(solution)/shard_map/convert_element_type | solution.py:35
  146.4 3.6 copy.58
  150.3 1.0 fusion.26
  151.4 2.6 fusion.70
  154.1 1.0 fusion.27
  155.0 1.2 copy.47
  156.3 2.8 fusion.71
  159.6 1.6 multiply_convert_fusion
  161.1 73.8 %all-gather.10.cloned.1.call-done = bf16[768,3072]{1,0:T(8,128)(2,1)} async-done(((bf16[96,3072]{1,0:T(8,128)(2,1)}), bf16[768,3072]{1,0:T(8,128)(2,1)}) %all-gather.10.cloned.1.call-update) | async-done | bytes 4718608 | tf_op jit(solution)/shard_map/all_gather | solution.py:54
  234.9 79.8 %all-gather.12.cloned.1.call-done = bf16[3072,768]{1,0:T(8,128)(2,1)} async-done(((bf16[384,768]{1,0:T(8,128)(2,1)}), bf16[3072,768]{1,0:T(8,128)(2,1)}) %all-gather.12.cloned.1.call-update) | async-done | bytes 4718608 | tf_op jit(solution)/shard_map/all_gather | solution.py:55
  314.7 51.6 %fusion.72 = (f32[1024]{0:T(1024)S(1)}, f32[1024,768]{0,1:T(8,128)S(1)}) fusion(bf16[3072,768]{1,0:T(8,128)(2,1)} %all-gather.12.cloned.1.call-done, bf16[1024,768]{0,1:T(8,128)(2,1)} %multiply_convert_fusion, bf16[768,3072]{1,0:T(8,128)(2,1)} %all-gather.10.cloned.1.call-done), kind=kOutput, calls=%fused_computation.120 | convolution fusion | flops 9870507008 | bytes 14159872 | tf_op jit(solution)/shard_map/dot_general | solution.py:61
  367.1 0.7 copy.60
  367.8 0.9 multiply_reduce_fusion
  368.9 6.3 %all-gather.14.cloned.1.call-done = bf16[2,768,1024]{2,1,0:T(8,128)(2,1)} async-done(((bf16[2,96,1024]{2,1,0:T(8,128)(2,1)}), bf16[2,768,1024]{2,1,0:T(8,128)(2,1)}) %all-gather.14.cloned.1.call-update) | async-done | bytes 3145744 | tf_op jit(solution)/shard_map/all_gather | solution.py:124
  375.1 2.5 fusion.25
  377.7 1.2 fusion.73
  379.2 1.3 multiply_convert_fusion.1
  (57 shorter events, 4.5 us)
Async XLA Ops:
  7.2 12.3 %copy-start = (bf16[512,768]{1,0:T(8,128)(2,1)S(1)}, bf16[512,768]{1,0:T(8,128)(2,1)}, u32[]{:S(2)}) copy-start(bf16[512,768]{1,0:T(8,128)(2,1)} %param.22) | copy-start | bytes 2359300
  7.2 123.9 %all-gather.6.cloned.1.call-start = ((), (), s32[]{:S(2)}) async-start(), calls=%async_computation.2 | async-start | bytes 3981312 | tf_op jit(solution)/shard_map/all_gather | solution.py:32
  7.9 148.4 %all-gather.8.cloned.1.call-start = ((), (), s32[]{:S(2)}) async-start(), calls=%async_computation.3 | async-start | bytes 1327104 | tf_op jit(solution)/shard_map/all_gather | solution.py:33
  8.7 226.2 %all-gather.10.cloned.1.call-start = ((), (), s32[]{:S(2)}) async-start(), calls=%async_computation.4 | async-start | bytes 5308416 | tf_op jit(solution)/shard_map/all_gather | solution.py:54
  9.4 305.3 %all-gather.12.cloned.1.call-start = ((), (), s32[]{:S(2)}) async-start(), calls=%async_computation.5 | async-start | bytes 5308416 | tf_op jit(solution)/shard_map/all_gather | solution.py:55
  11.3 14.9 %all-to-all-start.1 = ((bf16[32,1,1]{2,1,0:T(2,128)(2,1)}), bf16[32,1,1]{2,1,0:T(2,128)(2,1)S(1)}, u32[]{:S(2)}, u32[]{:S(2)}) async-start(bf16[32,1,1]{2,1,0:T(2,128)(2,1)} %copy.50), calls=%async_computation.1 | async-start | bytes 32768 | tf_op jit(solution)/shard_map/all_to_all | solution.py:105
  19.5 5.0 %copy-start.3 = (s32[1,32,48]{2,1,0:T(8,128)S(1)}, s32[1,32,48]{2,1,0:T(8,128)}, u32[]{:S(2)}) copy-start(s32[1,32,48]{2,1,0:T(8,128)} %param.23) | copy-start | bytes 18436
  26.2 92.0 %all-to-all-start = ((bf16[32,48,768]{2,1,0:T(8,128)(2,1)}), bf16[32,48,768]{2,1,0:T(8,128)(2,1)S(1)}, u32[]{:S(2)}, u32[]{:S(2)}) async-start(bf16[32,48,768]{2,1,0:T(8,128)(2,1)} %broadcast_select_fusion), calls=%async_computation | async-start | bytes 4718592 | tf_op jit(solution)/shard_map/all_to_all | solution.py:104
  32.1 3.2 copy-start.7
  32.1 3.3 copy-start.4
  32.1 343.0 %all-gather.14.cloned.1.call-start = ((), (), s32[]{:S(2)}) async-start(), calls=%async_computation.6 | async-start | bytes 3538944 | tf_op jit(solution)/shard_map/all_gather | solution.py:124
  154.1 2.3 copy-start.2
  156.3 3.2 copy-start.8
  161.1 205.5 %copy-start.9 = (f32[768]{0:T(1024)S(1)}, f32[768]{0:T(1024)}, u32[]{:S(2)}) copy-start(f32[768]{0:T(1024)} %param.21) | copy-start | bytes 9220
  367.8 7.3 %slice-start = ((bf16[512,768]{1,0:T(8,128)(2,1)}), bf16[504,768]{1,0:T(8,128)(2,1)S(1)}, s32[]{:S(2)}) async-start(bf16[512,768]{1,0:T(8,128)(2,1)} %param.22), calls=%async_computation.7 | async-start | bytes 1548288 | tf_op jit(solution)/shard_map/slice | solution.py:123
  368.7 9.0 %copy-start.1 = (f32[512,768]{1,0:T(8,128)S(1)}, f32[512,768]{1,0:T(8,128)}, u32[]{:S(2)}) copy-start(f32[512,768]{1,0:T(8,128)} %scatter_custom_fusion) | copy-start | bytes 4718596
  368.9 10.0 %copy-start.5 = (bf16[8,768]{1,0:T(8,128)(2,1)}, bf16[8,768]{1,0:T(8,128)(2,1)S(1)}, u32[]{:S(2)}) copy-start(bf16[8,768]{1,0:T(8,128)(2,1)S(1)} %copy.51) | copy-start | bytes 36868
  375.1 2.6 copy-start.10
  377.7 1.6 copy-start.6
Sparse Core Ops, SparseCore 0:
  10.2 103.0 all-gather.5
  115.4 39.1 all-gather.7
  156.9 78.0 all-gather.9
  236.9 77.6 all-gather.11
  316.7 58.3 all-gather.13
where the time goes:
time: 393 us; the launch traced here: 387 us
  waiting for transfers between devices  234 us (60%)
  matrix products  68.7 us (17%)
  other arithmetic  36 us (9%)
  local copies, waits for them, and re-layouts  21.3 us (5%)
  between operations  14.3 us (4%)
  starting transfers between devices  13.4 us (3%)
    all_gather x1, waiting for transfers between devices, encode_titles(): lax.all_gather(down_weight, 'fsdp', axis=0, tiled=True)  79.8 us
    all_gather x1, waiting for transfers between devices, encode_titles(): lax.all_gather(up_weight, 'fsdp', axis=0, tiled=True)  73.8 us
    all_to_all x1, waiting for transfers between devices, on_device(): lax.all_to_all(outgoing, ('fsdp', 'dom'), split_axis=0, concat_axis=0, ti...  70.7 us
    dot_general x1, matrix products, encode_titles(): lowered = jnp.dot(inner, full_down, preferred_element_type=jnp.float32)  51.6 us
    scatter-add x1, other arithmetic, scatter_sums(): sums = jax.ops.segment_sum(rows, label_flat, num_segments=nodes)  12.9 us
    scatter-add x1, other arithmetic, scatter_sums(): degree = jax.ops.segment_sum(mask_flat, label_flat, num_segments=nodes)  11.1 us
    dot_general x1, matrix products, encode_titles(): jnp.dot(flat, full_project, preferred_element_type=jnp.float32)  8.55 us
  transfers between devices with their start and end apart: 7, of which 4 were waited for; matrix products, arithmetic and copies ran while one was open for 31% of the time, Pallas kernels for 0%

commit v1 on v0

--- a/solution.py
+++ b/solution.py
@@ -7,6 +7,18 @@
 HEADS = 12
 HEAD_DIM = 64
 LN_EPSILON = 1e-12
+
+
+def collect(array, axis, dim):
+    ways, here, step = (lax.axis_size(axis), lax.axis_index(axis), array.shape[dim])
+    shape = [n * ways if d == dim else n for d, n in enumerate(array.shape)]
+    full = lax.dynamic_update_slice_in_dim(
+        jnp.zeros(shape, array.dtype), array, here * step, axis=dim
+    )
+    for far in range(1, ways):
+        array = lax.ppermute(array, axis, [(d, (d + 1) % ways) for d in range(ways)])
+        full = lax.dynamic_update_slice_in_dim(full, array, (here - far) % ways * step, axis=dim)
+    return full
 
 
 def layer_norm(values, gain):
@@ -52,7 +64,7 @@
     attended = lax.optimization_barrier(attended)
     full_up, full_down = (
         lax.all_gather(up_weight, "fsdp", axis=0, tiled=True),
-        lax.all_gather(down_weight, "fsdp", axis=0, tiled=True),
+        collect(down_weight, "fsdp", 0),
     )
     inner = jax.nn.gelu(
         jnp.dot(attended, full_up, preferred_element_type=jnp.float32), approximate=False

time: 393 us -> 377 us (0.959)
  waiting for transfers between devices: 234 us -> 204 us
  local copies, waits for them, and re-layouts: 21.3 us -> 38.6 us
  matrix products: 68.7 us -> 56.8 us
  starting transfers between devices: 13.4 us -> 19.7 us
    ppermute x0 -> x7, waiting for transfers between devices: none -> 182 us  [collect(): lax.ppermute(array, axis, [(d, (d + 1) % ways) for d in range(ways)])]
    all_gather x1 -> x0, waiting for transfers between devices: 79.8 us -> none  [encode_titles(): lax.all_gather(down_weight, 'fsdp', axis=0, tiled=True)]
    all_gather x1, waiting for transfers between devices: 73.8 us -> 2.44 us  [encode_titles(): lax.all_gather(up_weight, 'fsdp', axis=0, tiled=True)]
    all_to_all x1, waiting for transfers between devices: 70.7 us -> 0.01 us  [on_device(): lax.all_to_all(outgoing, ('fsdp', 'dom'), split_axis=0, concat_axis=0, ti...]
    dynamic_update_slice x0 -> x8, local copies, waits for them, and re-layouts: none -> 12.3 us  [the longest x7 11.4 us: collect(): lax.dynamic_update_slice_in_dim(full, array, (here - far) % ways * step,...]
    dot_general x1, matrix products: 51.6 us -> 39.8 us  [encode_titles(): lowered = jnp.dot(inner, full_down, preferred_element_type=jnp.float32)]
    all_gather x1, waiting for transfers between devices: 6.25 us -> 18 us  [on_device(): piece = lax.all_gather(sage_weight, 'fsdp', axis=1, tiled=True)]
    ppermute x0 -> x7, starting transfers between devices: none -> 6.41 us  [collect(): lax.ppermute(array, axis, [(d, (d + 1) % ways) for d in range(ways)])]
  transfers between devices with their start and end apart: 7 -> 13, of which waited for: 4 -> 9; matrix products, arithmetic and copies ran while one was open for 31% -> 33% of each run, Pallas kernels for 0% -> 0%
where the time goes in v1:
time: 377 us; the launch traced here: 370 us
  waiting for transfers between devices  204 us (54%)
  matrix products  56.8 us (15%)
  local copies, waits for them, and re-layouts  38.6 us (10%)
  other arithmetic  35.8 us (9%)
  starting transfers between devices  19.7 us (5%)
  between operations  14.7 us (4%)
    ppermute x7, waiting for transfers between devices, collect(): lax.ppermute(array, axis, [(d, (d + 1) % ways) for d in range(ways)])  182 us
    dot_general x1, matrix products, encode_titles(): lowered = jnp.dot(inner, full_down, preferred_element_type=jnp.float32)  39.8 us
    all_gather x1, waiting for transfers between devices, on_device(): piece = lax.all_gather(sage_weight, 'fsdp', axis=1, tiled=True)  18 us
    scatter-add x1, other arithmetic, scatter_sums(): sums = jax.ops.segment_sum(rows, label_flat, num_segments=nodes)  12.7 us
    dynamic_update_slice x7, local copies, waits for them, and re-layouts, collect(): lax.dynamic_update_slice_in_dim(full, array, (here - far) % ways * step,...  11.4 us
    scatter-add x1, other arithmetic, scatter_sums(): degree = jax.ops.segment_sum(mask_flat, label_flat, num_segments=nodes)  11.1 us
    dot_general x1, matrix products, encode_titles(): jnp.dot(flat, full_project, preferred_element_type=jnp.float32)  8.48 us
  transfers between devices with their start and end apart: 13, of which 9 were waited for; matrix products, arithmetic and copies ran while one was open for 33% of the time, Pallas kernels for 0%

profile of v1, /device:TPU:0, one launch (start us, length us, event | category | flops | bytes accessed | tf_op | source)
XLA Modules:
  0.0 369.7 jit_solution(4443884126761243739)
XLA Ops:
  10.8 7.3 %all-to-all-start.1 = ((bf16[32,1,1]{2,1,0:T(2,128)(2,1)}), bf16[32,1,1]{2,1,0:T(2,128)(2,1)S(1)}, u32[]{:S(2)}, u32[]{:S(2)}) async-start(bf16[32,1,1]{2,1,0:T(2,128)(2,1)} %copy.50), calls=%async_computation.1 | async-start | bytes 32768 | tf_op jit(solution)/shard_map/all_to_all | solution.py:117
  18.9 5.0 %gather_fusion = bf16[1536,768]{1,0:T(8,128)(2,1)S(1)} fusion(bf16[512,768]{1,0:T(8,128)(2,1)S(1)} %copy-done, s32[2048]{0:T(1024)S(1)} %pad_clamp_fusion), kind=kCustom, calls=%fused_computation | custom fusion | bytes 4724736 | tf_op jit(solution)/shard_map/jit(_take)/gather | solution.py:112
  23.9 1.7 broadcast_select_fusion
  25.7 5.8 %all-to-all-start = ((bf16[32,48,768]{2,1,0:T(8,128)(2,1)}), bf16[32,48,768]{2,1,0:T(8,128)(2,1)S(1)}, u32[]{:S(2)}, u32[]{:S(2)}) async-start(bf16[32,48,768]{2,1,0:T(8,128)(2,1)} %broadcast_select_fusion), calls=%async_computation | async-start | bytes 4718592 | tf_op jit(solution)/shard_map/all_to_all | solution.py:116
  31.6 1.8 collective-permute-start
  33.4 86.7 %collective-permute-done = bf16[384,768]{1,0:T(8,128)(2,1)S(1)} collective-permute-done((bf16[384,768]{1,0:T(8,128)(2,1)}, bf16[384,768]{1,0:T(8,128)(2,1)S(1)}, u32[]{:S(2)}, u32[]{:S(2)}) %collective-permute-start) | collective-permute-done | bytes 589856 | tf_op jit(solution)/shard_map/ppermute | solution.py:19
  120.9 17.0 %collective-permute-done.1 = bf16[384,768]{1,0:T(8,128)(2,1)S(1)} collective-permute-done((bf16[384,768]{1,0:T(8,128)(2,1)S(1)}, bf16[384,768]{1,0:T(8,128)(2,1)S(1)}, u32[]{:S(2)}, u32[]{:S(2)}) %collective-permute-start.1) | collective-permute-done | bytes 589856 | tf_op jit(solution)/shard_map/ppermute | solution.py:19
  138.7 20.5 %collective-permute-done.2 = bf16[384,768]{1,0:T(8,128)(2,1)S(1)} collective-permute-done((bf16[384,768]{1,0:T(8,128)(2,1)S(1)}, bf16[384,768]{1,0:T(8,128)(2,1)S(1)}, u32[]{:S(2)}, u32[]{:S(2)}) %collective-permute-start.2) | collective-permute-done | bytes 589856 | tf_op jit(solution)/shard_map/ppermute | solution.py:19
  160.0 2.6 collective-permute-start.3
  162.6 11.7 %collective-permute-done.3 = bf16[384,768]{1,0:T(8,128)(2,1)} collective-permute-done((bf16[384,768]{1,0:T(8,128)(2,1)S(1)}, bf16[384,768]{1,0:T(8,128)(2,1)}, u32[]{:S(2)}, u32[]{:S(2)}) %collective-permute-start.3) | collective-permute-done | bytes 589856 | tf_op jit(solution)/shard_map/ppermute | solution.py:19
  174.3 2.0 collective-permute-start.4
  176.4 2.7 copy.54
  179.3 2.5 broadcast_in_dim.30
  182.8 20.8 %collective-permute-done.4 = bf16[384,768]{1,0:T(8,128)(2,1)} collective-permute-done((bf16[384,768]{1,0:T(8,128)(2,1)}, bf16[384,768]{1,0:T(8,128)(2,1)}, u32[]{:S(2)}, u32[]{:S(2)}) %collective-permute-start.4) | collective-permute-done | bytes 589856 | tf_op jit(solution)/shard_map/ppermute | solution.py:19
  204.4 11.1 %scatter_custom_fusion.1 = f32[512]{0:T(512)S(1)} fusion(s32[1536]{0:T(1024)S(1)} %reshape.151, f32[1536]{0:T(1024)S(1)} %reshape.161, f32[]{:T(128)} %constant.56.clone.1), kind=kCustom, calls=%fused_computation.89 | custom fusion | flops 1536 | bytes 2052 | tf_op jit(solution)/shard_map/scatter-add | solution.py:90
  215.6 1.9 constant_dynamic-update-slice_fusion.6
  217.5 5.8 %collective-permute-done.5 = bf16[384,768]{1,0:T(8,128)(2,1)S(1)} collective-permute-done((bf16[384,768]{1,0:T(8,128)(2,1)}, bf16[384,768]{1,0:T(8,128)(2,1)S(1)}, u32[]{:S(2)}, u32[]{:S(2)}) %collective-permute-start.5) | collective-permute-done | bytes 589856 | tf_op jit(solution)/shard_map/ppermute | solution.py:19
  223.3 2.0 constant_dynamic-update-slice_fusion.5
  225.3 1.9 constant_dynamic-update-slice_fusion.4
  227.3 1.9 constant_dynamic-update-slice_fusion.3
  229.2 1.9 constant_dynamic-update-slice_fusion.2
  231.9 19.0 %collective-permute-done.6 = bf16[384,768]{1,0:T(8,128)(2,1)S(1)} collective-permute-done((bf16[384,768]{1,0:T(8,128)(2,1)S(1)}, bf16[384,768]{1,0:T(8,128)(2,1)S(1)}, u32[]{:S(2)}, u32[]{:S(2)}) %collective-permute-start.6) | collective-permute-done | bytes 589856 | tf_op jit(solution)/shard_map/ppermute | solution.py:19
  251.8 12.7 %scatter_custom_fusion = f32[512,768]{1,0:T(8,128)} fusion(s32[1536]{0:T(1024)S(1)} %reshape.151, bf16[1536,768]{1,0:T(8,128)(2,1)S(1)} %bitcast.72, f32[1536]{0:T(1024)S(1)} %reshape.161, f32[]{:T(128)} %constant.56.clone.1), kind=kCustom, calls=%fused_computation.30 | custom fusion | flops 3538944 | bytes 3940356 | tf_op jit(solution)/shard_map/scatter-add | solution.py:89
  264.5 8.5 %convolution_convert_fusion = bf16[1024,2304]{1,0:T(8,128)(2,1)} fusion(bf16[1024,768]{1,0:T(8,128)(2,1)} %bitcast.74, bf16[768,2304]{1,0:T(8,128)(2,1)} %all-gather.5.cloned.1.call-done), kind=kOutput, calls=%fused_computation.27 | convolution fusion | flops 3626237952 | bytes 9830400 | tf_op jit(solution)/shard_map/dot_general | solution.py:47
  273.0 6.7 %copy.42 = bf16[1024,2304]{0,1:T(8,128)(2,1)} copy(bf16[1024,2304]{1,0:T(8,128)(2,1)} %convolution_convert_fusion) | data formatting | bytes 9437184 | tf_op jit(solution)/shard_map/convert_element_type | solution.py:47
  279.6 3.6 copy.58
  284.6 2.6 fusion.70
  289.6 2.8 fusion.71
  294.4 2.4 all-gather.9.cloned.1.call-done
  296.8 39.8 %fusion.72 = (f32[1024]{0:T(1024)S(1)}, f32[1024,768]{0,1:T(8,128)S(1)}) fusion(bf16[3072,768]{1,0:T(8,128)(2,1)} %constant_dynamic-update-slice_fusion, bf16[1024,768]{0,1:T(8,128)(2,1)} %multiply_convert_fusion, bf16[768,3072]{1,0:T(8,128)(2,1)} %all-gather.9.cloned.1.call-done), kind=kOutput, calls=%fused_computation.128 | convolution fusion | flops 9870507008 | bytes 14159872 | tf_op jit(solution)/shard_map/dot_general | solution.py:73
  339.3 18.0 %all-gather.11.cloned.1.call-done = bf16[2,768,1024]{2,1,0:T(8,128)(2,1)} async-done(((bf16[2,96,1024]{2,1,0:T(8,128)(2,1)}), bf16[2,768,1024]{2,1,0:T(8,128)(2,1)}) %all-gather.11.cloned.1.call-update) | async-done | bytes 3145744 | tf_op jit(solution)/shard_map/all_gather | solution.py:136
  357.3 2.5 fusion.25
  (85 shorter events, 21.6 us)
Async XLA Ops:
  7.2 11.7 %copy-start = (bf16[512,768]{1,0:T(8,128)(2,1)S(1)}, bf16[512,768]{1,0:T(8,128)(2,1)}, u32[]{:S(2)}) copy-start(bf16[512,768]{1,0:T(8,128)(2,1)} %param.22) | copy-start | bytes 2359300
  7.2 257.3 %all-gather.5.cloned.1.call-start = ((), (), s32[]{:S(2)}) async-start(), calls=%async_computation.2 | async-start | bytes 3981312 | tf_op jit(solution)/shard_map/all_gather | solution.py:44
  7.9 281.6 %all-gather.7.cloned.1.call-start = ((), (), s32[]{:S(2)}) async-start(), calls=%async_computation.3 | async-start | bytes 1327104 | tf_op jit(solution)/shard_map/all_gather | solution.py:45
  8.7 288.2 %all-gather.9.cloned.1.call-start = ((), (), s32[]{:S(2)}) async-start(), calls=%async_computation.4 | async-start | bytes 5308416 | tf_op jit(solution)/shard_map/all_gather | solution.py:66
  10.8 14.9 %all-to-all-start.1 = ((bf16[32,1,1]{2,1,0:T(2,128)(2,1)}), bf16[32,1,1]{2,1,0:T(2,128)(2,1)S(1)}, u32[]{:S(2)}, u32[]{:S(2)}) async-start(bf16[32,1,1]{2,1,0:T(2,128)(2,1)} %copy.50), calls=%async_computation.1 | async-start | bytes 32768 | tf_op jit(solution)/shard_map/all_to_all | solution.py:117
  18.9 5.0 %copy-start.7 = (s32[1,32,48]{2,1,0:T(8,128)S(1)}, s32[1,32,48]{2,1,0:T(8,128)}, u32[]{:S(2)}) copy-start(s32[1,32,48]{2,1,0:T(8,128)} %param.23) | copy-start | bytes 18436
  25.7 153.4 %copy-start.11 = (s32[8,128]{1,0:T(8,128)S(1)}, s32[8,128]{1,0:T(8,128)}, u32[]{:S(2)}) copy-start(s32[8,128]{1,0:T(8,128)} %param.15) | copy-start | bytes 12292
  25.7 153.6 %copy-start.8 = (s32[1,32,48]{2,1,0:T(8,128)S(1)}, s32[1,32,48]{2,1,0:T(8,128)}, u32[]{:S(2)}) copy-start(s32[1,32,48]{2,1,0:T(8,128)} %param.25) | copy-start | bytes 18436
  25.7 226.1 %all-to-all-start = ((bf16[32,48,768]{2,1,0:T(8,128)(2,1)}), bf16[32,48,768]{2,1,0:T(8,128)(2,1)S(1)}, u32[]{:S(2)}, u32[]{:S(2)}) async-start(bf16[32,48,768]{2,1,0:T(8,128)(2,1)} %broadcast_select_fusion), calls=%async_computation | async-start | bytes 4718592 | tf_op jit(solution)/shard_map/all_to_all | solution.py:116
  31.5 325.8 %all-gather.11.cloned.1.call-start = ((), (), s32[]{:S(2)}) async-start(), calls=%async_computation.5 | async-start | bytes 3538944 | tf_op jit(solution)/shard_map/all_gather | solution.py:136
  31.6 88.5 %collective-permute-start = (bf16[384,768]{1,0:T(8,128)(2,1)}, bf16[384,768]{1,0:T(8,128)(2,1)S(1)}, u32[]{:S(2)}, u32[]{:S(2)}) collective-permute-start(bf16[384,768]{1,0:T(8,128)(2,1)} %param.19), channel_id=1, source_target_pairs={{0,4},{4,8},{8,12},{12,16},{16,20},{20,24},{24,28},{28,0},{1,5},{5... | collective-permute-start | bytes 1769480 | tf_op jit(solution)/shard_map/ppermute | solution.py:19
  120.1 0.8 copy-start.6
  120.1 17.8 %collective-permute-start.1 = (bf16[384,768]{1,0:T(8,128)(2,1)S(1)}, bf16[384,768]{1,0:T(8,128)(2,1)S(1)}, u32[]{:S(2)}, u32[]{:S(2)}) collective-permute-start(bf16[384,768]{1,0:T(8,128)(2,1)S(1)} %collective-permute-done), channel_id=1, source_target_pairs={{0,4},{4,8},{8,12},{12,16},{16,20},{20,24},{24,28},{28,0},{1,5},{5... | collective-permute-start | bytes 1769480 | tf_op jit(solution)/shard_map/ppermute | solution.py:19
  137.9 0.8 copy-start.4
  138.7 20.5 %collective-permute-start.2 = (bf16[384,768]{1,0:T(8,128)(2,1)S(1)}, bf16[384,768]{1,0:T(8,128)(2,1)S(1)}, u32[]{:S(2)}, u32[]{:S(2)}) collective-permute-start(bf16[384,768]{1,0:T(8,128)(2,1)S(1)} %collective-permute-done.1), channel_id=1, source_target_pairs={{0,4},{4,8},{8,12},{12,16},{16,20},{20,24},{24,28},{28,0},{1,5},{5... | collective-permute-start | bytes 1769480 | tf_op jit(solution)/shard_map/ppermute | solution.py:19
  159.2 0.8 copy-start.5
  160.0 14.2 %collective-permute-start.3 = (bf16[384,768]{1,0:T(8,128)(2,1)S(1)}, bf16[384,768]{1,0:T(8,128)(2,1)}, u32[]{:S(2)}, u32[]{:S(2)}) collective-permute-start(bf16[384,768]{1,0:T(8,128)(2,1)S(1)} %collective-permute-done.2), channel_id=1, source_target_pairs={{0,4},{4,8},{8,12},{12,16},{16,20},{20,24},{24,28},{28,0},{1,5},{5... | collective-permute-start | bytes 1769480 | tf_op jit(solution)/shard_map/ppermute | solution.py:19
  174.3 29.3 %collective-permute-start.4 = (bf16[384,768]{1,0:T(8,128)(2,1)}, bf16[384,768]{1,0:T(8,128)(2,1)}, u32[]{:S(2)}, u32[]{:S(2)}) collective-permute-start(bf16[384,768]{1,0:T(8,128)(2,1)} %collective-permute-done.3), channel_id=1, source_target_pairs={{0,4},{4,8},{8,12},{12,16},{16,20},{20,24},{24,28},{28,0},{1,5},{5... | collective-permute-start | bytes 1769480 | tf_op jit(solution)/shard_map/ppermute | solution.py:19
  176.4 5.5 %copy-start.3 = (bf16[384,768]{1,0:T(8,128)(2,1)S(1)}, bf16[384,768]{1,0:T(8,128)(2,1)}, u32[]{:S(2)}) copy-start(bf16[384,768]{1,0:T(8,128)(2,1)} %param.19) | copy-start | bytes 1769476
  203.6 19.7 %collective-permute-start.5 = (bf16[384,768]{1,0:T(8,128)(2,1)}, bf16[384,768]{1,0:T(8,128)(2,1)S(1)}, u32[]{:S(2)}, u32[]{:S(2)}) collective-permute-start(bf16[384,768]{1,0:T(8,128)(2,1)} %collective-permute-done.4), channel_id=1, source_target_pairs={{0,4},{4,8},{8,12},{12,16},{16,20},{20,24},{24,28},{28,0},{1,5},{5... | collective-permute-start | bytes 1769480 | tf_op jit(solution)/shard_map/ppermute | solution.py:19
  223.3 27.6 %collective-permute-start.6 = (bf16[384,768]{1,0:T(8,128)(2,1)S(1)}, bf16[384,768]{1,0:T(8,128)(2,1)S(1)}, u32[]{:S(2)}, u32[]{:S(2)}) collective-permute-start(bf16[384,768]{1,0:T(8,128)(2,1)S(1)} %collective-permute-done.5), channel_id=1, source_target_pairs={{0,4},{4,8},{8,12},{12,16},{16,20},{20,24},{24,28},{28,0},{1,5},{5... | collective-permute-start | bytes 1769480 | tf_op jit(solution)/shard_map/ppermute | solution.py:19
  287.3 2.3 copy-start.1
  289.6 3.2 copy-start.12
  294.4 42.6 %copy-start.13 = (f32[768]{0:T(1024)S(1)}, f32[768]{0:T(1024)}, u32[]{:S(2)}) copy-start(f32[768]{0:T(1024)} %param.21) | copy-start | bytes 9220
  337.4 19.9 %slice-start = ((bf16[512,768]{1,0:T(8,128)(2,1)}), bf16[504,768]{1,0:T(8,128)(2,1)S(1)}, s32[]{:S(2)}) async-start(bf16[512,768]{1,0:T(8,128)(2,1)} %param.22), calls=%async_computation.6 | async-start | bytes 1548288 | tf_op jit(solution)/shard_map/slice | solution.py:135
  338.2 21.6 %copy-start.2 = (f32[512,768]{1,0:T(8,128)S(1)}, f32[512,768]{1,0:T(8,128)}, u32[]{:S(2)}) copy-start(f32[512,768]{1,0:T(8,128)} %scatter_custom_fusion) | copy-start | bytes 4718596
  339.3 21.8 %copy-start.9 = (bf16[8,768]{1,0:T(8,128)(2,1)}, bf16[8,768]{1,0:T(8,128)(2,1)S(1)}, u32[]{:S(2)}) copy-start(bf16[8,768]{1,0:T(8,128)(2,1)S(1)} %copy.51) | copy-start | bytes 36868
  357.3 2.6 copy-start.14
  359.9 1.6 copy-start.10
Sparse Core Ops, SparseCore 0:
  10.2 103.0 all-gather.4
  115.4 82.3 all-gather.6
  200.0 96.7 all-gather.8
  298.9 58.3 all-gather.10
